TPU v7x, 32 devices: a whole 2x2x4 slice. The times are simulated.
32 devices in a mesh: dp: 8 (over z, y), mp: 4 (over x, core).
Axes of the slice: x: 2, y: 2, z: 4, core: 2. Of those that a mesh axis runs over, the one named last changes fastest.
Arguments:
- hidden_input: bfloat16 [8192, 24], P('dp'), may hold values from -6 to 6
- output_cotangent: bfloat16 [8192, 8192], P('dp', 'mp'), may hold values from -0.023925781 to 0.023925781
- master_weights: float32 [24, 8192], P('dp', 'mp'), may hold values from -6 to 6
- first_codes: int32 [24, 8192], P('dp', 'mp'), may hold values from 0 to 15
- second_codes: int32 [24, 8192], P('dp', 'mp'), may hold values from 0 to 15
- first_rows: float32 [24], P('dp'), may hold values from 0.001 to 0.03
- first_cols: float32 [8192], P('mp'), may hold values from 0.001 to 0.03
- second_rows: float32 [24], P('dp'), may hold values from 1e-05 to 0.001
- second_cols: float32 [8192], P('mp'), may hold values from 1e-05 to 0.001
- step_count: int32 [], replicated, may hold values from 1 to 9
Outputs:
- new_master: float32 [24, 8192], P('dp', 'mp')
- update_ratio: float32 [24, 8192], P('dp', 'mp')
- gathered_params: bfloat16 [24, 8192], P(None, 'mp')
- first_scaled: float32 [24, 8192], P('dp', 'mp')
- second_scaled: float32 [24, 8192], P('dp', 'mp')
- new_first_rows: float32 [24], P('dp')
- new_first_cols: float32 [8192], P('mp')
- new_second_rows: float32 [24], P('dp')
- new_second_cols: float32 [8192], P('mp')
All inputs are finite; a program needn't handle non-finite values.
Results may differ from a plain program's by a relative error of at most 0.001.
Values may be sent and summed in bfloat16 or wider, within the bound.
A program may use at most 64 MiB of HBM per device.

v0:
```python
import jax
import jax.numpy as jnp
from jax import lax
from jax.sharding import PartitionSpec as P


def shards(
    hidden_input,
    output_cotangent,
    master_weights,
    first_codes,
    second_codes,
    first_rows,
    first_cols,
    second_rows,
    second_cols,
    step_count,
):
    local_rows = master_weights.shape[0]
    local_cols = master_weights.shape[1]
    whole_term = jnp.dot(hidden_input.T, output_cotangent, preferred_element_type=jnp.float32)
    column_share = lax.psum_scatter(whole_term, "dp", scatter_dimension=1, tiled=True)
    gradient = lax.all_to_all(column_share, "dp", split_axis=0, concat_axis=1, tiled=True)
    squares = lax.psum(jnp.sum(gradient * gradient), ("dp", "mp"))
    entries = local_rows * local_cols * lax.axis_size("dp") * lax.axis_size("mp")
    clipf = jnp.minimum(1.0, 0.01 * jnp.sqrt(jnp.float32(entries)) / (jnp.sqrt(squares) + 1e-06))
    clipped = clipf * gradient
    first_old = (
        (first_codes.astype(jnp.float32) - 7.5)
        / 7.5
        * jnp.minimum(first_rows[:, None], first_cols[None, :])
    )
    second_level = (second_codes.astype(jnp.float32) + 1.0) / 16.0
    second_old = (
        second_level * second_level * jnp.minimum(second_rows[:, None], second_cols[None, :])
    )
    first_new = 0.9 * first_old + 0.1 * clipped
    second_new = 0.95 * second_old + 0.05 * clipped * clipped
    steps = step_count.astype(jnp.float32)
    first_fix = 1.0 - jnp.power(jnp.float32(0.9), steps)
    second_fix = 1.0 - jnp.power(jnp.float32(0.95), steps)
    update_ratio = first_new / first_fix / (jnp.sqrt(second_new / second_fix) + 1e-08)
    new_master = master_weights - 0.001 * (update_ratio + 0.1 * master_weights)
    gathered_params = lax.all_gather(new_master.astype(jnp.bfloat16), "dp", axis=0, tiled=True)
    first_abs = jnp.abs(first_new)
    first_rowpart = jnp.max(first_abs, axis=1)
    first_colpart = jnp.max(first_abs, axis=0)
    second_rowpart = jnp.max(second_new, axis=1)
    second_colpart = jnp.max(second_new, axis=0)
    new_first_rows, new_second_rows = lax.pmax((first_rowpart, second_rowpart), "mp")
    new_first_cols, new_second_cols = lax.pmax((first_colpart, second_colpart), "dp")
    first_scaled = first_new / (
        jnp.minimum(new_first_rows[:, None], new_first_cols[None, :]) + 1e-08
    )
    second_scaled = second_new / (
        jnp.minimum(new_second_rows[:, None], new_second_cols[None, :]) + 1e-08
    )
    return (
        new_master,
        update_ratio,
        gathered_params,
        first_scaled,
        second_scaled,
        new_first_rows,
        new_first_cols,
        new_second_rows,
        new_second_cols,
    )


def solution(mesh):
    return jax.shard_map(
        shards,
        mesh=mesh,
        in_specs=(
            P("dp", None),
            P("dp", "mp"),
            P("dp", "mp"),
            P("dp", "mp"),
            P("dp", "mp"),
            P("dp"),
            P("mp"),
            P("dp"),
            P("mp"),
            P(),
        ),
        out_specs=(
            P("dp", "mp"),
            P("dp", "mp"),
            P(None, "mp"),
            P("dp", "mp"),
            P("dp", "mp"),
            P("dp"),
            P("mp"),
            P("dp"),
            P("mp"),
        ),
        check_vma=False,
    )
```

profile of v0, /device:TPU:0, one launch (start us, length us, event | category | flops | bytes accessed | tf_op | source)
XLA Modules:
  0.0 209.0 jit_solution(5620528497959128077)
XLA Ops:
  7.2 0.0 copy-start
  7.2 0.0 copy-start.4
  7.2 0.0 copy-start.8
  7.2 0.0 copy-start.5
  7.2 0.0 copy-start.9
  7.2 0.0 copy-start.1
  7.2 0.0 copy-start.2
  7.3 0.0 copy-start.3
  7.3 0.0 reduce-scatter.2.cloned.1.call-start
  7.3 0.7 copy-done
  8.0 3.5 %fusion.3 = f32[24,2048]{1,0:T(8,128)} fusion(bf16[1024,24]{0,1:T(8,128)(2,1)S(1)} %copy-done, bf16[1024,2048]{1,0:T(8,128)(2,1)} %param.11), kind=kOutput, calls=%fused_computation.13 | convolution fusion | flops 100663296 | bytes 4440064 | tf_op jit(solution)/shard_map/dot_general | solution.py:21
  11.5 0.0 reduce-scatter.2.cloned.1.call-update
  11.5 64.8 %reduce-scatter.2.cloned.1.call-done = f32[24,256]{1,0:T(8,128)} async-done(((f32[24,2048]{1,0:T(8,128)}), f32[24,256]{1,0:T(8,128)}) %reduce-scatter.2.cloned.1.call-update) | async-done | bytes 24592 | tf_op jit(solution)/shard_map/reduce_scatter | solution.py:22
  76.4 1.4 all_to_all.10
  77.7 3.6 %all-to-all-start = ((f32[8,3,256]{2,1,0:T(4,128)}), f32[8,3,256]{2,1,0:T(4,128)S(1)}, u32[]{:S(2)}, u32[]{:S(2)}) async-start(f32[8,3,256]{2,1,0:T(4,128)} %all_to_all.10), calls=%async_computation.1 | async-start | bytes 65536 | tf_op jit(solution)/shard_map/all_to_all | solution.py:23
  82.1 6.0 %all-to-all-done = f32[8,3,256]{2,1,0:T(4,128)S(1)} async-done(((f32[8,3,256]{2,1,0:T(4,128)}), f32[8,3,256]{2,1,0:T(4,128)S(1)}, u32[]{:S(2)}, u32[]{:S(2)}) %all-to-all-start) | async-done | bytes 24608 | tf_op jit(solution)/shard_map/all_to_all | solution.py:23
  88.0 0.6 multiply_reduce_fusion
  88.7 38.5 %psum.7 = f32[]{:T(128)} all-reduce(f32[]{:T(128)} %multiply_reduce_fusion), channel_id=1, replica_groups=mesh['dp'=8,'mp'=4] {'dp','mp'}, use_global_device_ids=true, to_apply=%region_2.0 | all-reduce | flops 1 | bytes 8 | tf_op jit(solution)/shard_map/psum | solution.py:24
  127.9 0.0 copy-done.4
  127.9 0.0 copy-done.8
  127.9 0.0 copy-done.5
  127.9 0.0 copy-done.9
  127.9 0.0 copy-done.1
  127.9 0.0 copy-done.2
  127.9 0.2 fusion.1
  128.2 6.5 %all-reduce.1 = (f32[3]{0:T(128)S(1)}, f32[3]{0:T(128)S(1)}) all-reduce(f32[3]{0:T(128)S(1)} %get-tuple-element.25, f32[3]{0:T(128)S(1)} %get-tuple-element.9), channel_id=1, replica_groups=mesh['dp'=8,'mp'=4] {'mp'}, use_global_device_ids=true, to_apply=%region_4.0 | all-reduce | flops 6 | bytes 48 | tf_op jit(solution)/shard_map/pmax | solution.py:50
  134.7 35.4 %all-reduce = (f32[2048]{0:T(1024)S(1)}, f32[2048]{0:T(1024)S(1)}) all-reduce(f32[2048]{0:T(1024)S(1)} %get-tuple-element.24, f32[2048]{0:T(1024)S(1)} %get-tuple-element.10), channel_id=1, replica_groups=mesh['dp'=8,'mp'=4] {'dp'}, use_global_device_ids=true, to_apply=%region_6.0 | all-reduce | flops 4096 | bytes 32768 | tf_op jit(solution)/shard_map/pmax | solution.py:51
  170.1 0.0 copy-done.3
  170.1 0.7 convert_bitcast_fusion
  170.9 30.5 %all-gather = bf16[8,3,2048]{2,1,0:T(4,128)(2,1)S(1)} all-gather(bf16[1,3,2048]{2,1,0:T(4,128)(2,1)S(1)} %get-tuple-element.19), channel_id=1, replica_groups=mesh['dp'=8,'mp'=4] {'dp'}, dimensions={0}, use_global_device_ids=true | all-gather | bytes 110592 | tf_op jit(solution)/shard_map/all_gather | solution.py:44
  201.4 0.7 reshape.32
  202.1 0.0 copy-done.11
  (8 shorter events, 0.0 us)
Async XLA Ops:
  7.2 0.8 copy-start
  7.2 120.7 %copy-start.4 = (f32[2048]{0:T(1024)S(1)}, f32[2048]{0:T(1024)}, u32[]{:S(2)}) copy-start(f32[2048]{0:T(1024)} %param.18) | copy-start | bytes 24580
  7.2 120.7 %copy-start.8 = (f32[3]{0:T(128)S(1)}, f32[3]{0:T(128)}, u32[]{:S(2)}) copy-start(f32[3]{0:T(128)} %param.17) | copy-start | bytes 40
  7.2 120.7 %copy-start.5 = (f32[2048]{0:T(1024)S(1)}, f32[2048]{0:T(1024)}, u32[]{:S(2)}) copy-start(f32[2048]{0:T(1024)} %param.16) | copy-start | bytes 24580
  7.2 120.7 %copy-start.9 = (f32[3]{0:T(128)S(1)}, f32[3]{0:T(128)}, u32[]{:S(2)}) copy-start(f32[3]{0:T(128)} %param.15) | copy-start | bytes 40
  7.2 120.7 %copy-start.1 = (s32[3,2048]{1,0:T(4,128)S(1)}, s32[3,2048]{1,0:T(4,128)}, u32[]{:S(2)}) copy-start(s32[3,2048]{1,0:T(4,128)} %param.14) | copy-start | bytes 73732
  7.2 120.7 %copy-start.2 = (s32[3,2048]{1,0:T(4,128)S(1)}, s32[3,2048]{1,0:T(4,128)}, u32[]{:S(2)}) copy-start(s32[3,2048]{1,0:T(4,128)} %param.13) | copy-start | bytes 73732
  7.3 162.9 %copy-start.3 = (f32[3,2048]{1,0:T(4,128)S(1)}, f32[3,2048]{1,0:T(4,128)}, u32[]{:S(2)}) copy-start(f32[3,2048]{1,0:T(4,128)} %param.12) | copy-start | bytes 73732
  7.3 69.1 %reduce-scatter.2.cloned.1.call-start = ((), (), s32[]{:S(2)}) async-start(), calls=%async_computation.2 | async-start | bytes 221184 | tf_op jit(solution)/shard_map/reduce_scatter | solution.py:22
  77.7 10.3 %all-to-all-start = ((f32[8,3,256]{2,1,0:T(4,128)}), f32[8,3,256]{2,1,0:T(4,128)S(1)}, u32[]{:S(2)}, u32[]{:S(2)}) async-start(f32[8,3,256]{2,1,0:T(4,128)} %all_to_all.10), calls=%async_computation.1 | async-start | bytes 65536 | tf_op jit(solution)/shard_map/all_to_all | solution.py:23
  134.7 67.4 %copy-start.10 = (f32[3]{0:T(128)}, f32[3]{0:T(128)S(1)}, u32[]{:S(2)}) copy-start(f32[3]{0:T(128)S(1)} %get-tuple-element.15) | copy-start | bytes 40
  134.7 67.4 %copy-start.11 = (f32[3]{0:T(128)}, f32[3]{0:T(128)S(1)}, u32[]{:S(2)}) copy-start(f32[3]{0:T(128)S(1)} %get-tuple-element.16) | copy-start | bytes 40
  170.1 32.0 %copy-start.6 = (f32[2048]{0:T(1024)}, f32[2048]{0:T(1024)S(1)}, u32[]{:S(2)}) copy-start(f32[2048]{0:T(1024)S(1)} %get-tuple-element.13) | copy-start | bytes 24580
  170.1 32.0 %copy-start.7 = (f32[2048]{0:T(1024)}, f32[2048]{0:T(1024)S(1)}, u32[]{:S(2)}) copy-start(f32[2048]{0:T(1024)S(1)} %get-tuple-element.14) | copy-start | bytes 24580
Sparse Core Ops, SparseCore 0:
  11.7 64.6 reduce-scatter.1
where the time goes:
time: 209 us
  blocking collectives  111 us (53%)
  waiting for transfers between devices  70.8 us (34%)
  between operations  15.7 us (8%)
  starting transfers between devices  3.65 us (2%)
  matrix products  3.52 us (2%)
  local copies, waits for them, and re-layouts  2.81 us (1%)
    reduce_scatter x1, waiting for transfers between devices, shards(): lax.psum_scatter(whole_term, 'dp', scatter_dimension=1, tiled=True)  64.8 us
    psum x1, blocking collectives, shards(): squares = lax.psum(jnp.sum(gradient * gradient), ('dp', 'mp'))  38.5 us
    pmax x1, blocking collectives, shards(): lax.pmax((first_colpart, second_colpart), 'dp')  35.4 us
    all_gather x1, blocking collectives, shards(): lax.all_gather(new_master.astype(jnp.bfloat16), 'dp', axis=0, tiled=True)  30.5 us
    pmax x1, blocking collectives, shards(): lax.pmax((first_rowpart, second_rowpart), 'mp')  6.54 us
    all_to_all x1, waiting for transfers between devices, shards(): lax.all_to_all(column_share, 'dp', split_axis=0, concat_axis=1, tiled=True)  5.95 us
  transfers between devices with their start and end apart: 2, of which 2 were waited for; matrix products, arithmetic and copies ran while one was open for 0% of the time, Pallas kernels for 0%

commit v1 on v0

v1 whole, which is shorter than its diff:
```python
import functools

import jax
import jax.numpy as jnp
from jax import lax
from jax.experimental import pallas as pl
from jax.experimental.pallas import tpu as pltpu
from jax.sharding import PartitionSpec as P

MESH = pl.DeviceIdType.MESH
F32 = jnp.float32


def kernel(
    ndp,
    nmp,
    chunks,
    hidden_hbm,
    cot_hbm,
    master_hbm,
    code1_hbm,
    code2_hbm,
    cols1_hbm,
    cols2_hbm,
    rows1_ref,
    rows2_ref,
    step_ref,
    master_out,
    ratio_out,
    params_out,
    scaled1_out,
    scaled2_out,
    rows_out,
    newcols1_out,
    newcols2_out,
    hidden,
    cot,
    master,
    code1,
    code2,
    cols1,
    cols2,
    share,
    grads,
    square,
    squares,
    params,
    maxcol,
    maxcols,
    maxrow,
    maxrows,
    old1,
    old2,
    in_sem,
    cot_sem,
    send_sem,
    recv_sem,
):
    dp = lax.axis_index("dp")
    mp = lax.axis_index("mp")
    ndev = ndp * nmp
    flat = dp * nmp + mp
    rows, ncols = master.shape
    width = ncols // chunks

    def loop(count, body):
        def step(i, carry):
            body(i)
            return carry

        lax.fori_loop(0, count, step, 0, unroll=count <= 32)

    loads = []
    for i, (src, dst) in enumerate(
        (
            (hidden_hbm, hidden),
            (code1_hbm, code1),
            (code2_hbm, code2),
            (cols1_hbm, cols1),
            (cols2_hbm, cols2),
            (master_hbm, master),
        )
    ):
        copy = pltpu.make_async_copy(src, dst, in_sem.at[i])
        loads.append(copy)
    cot_loads = [
        pltpu.make_async_copy(
            cot_hbm.at[:, pl.ds(c * width, width)], cot.at[c], cot_sem.at[c]
        )
        for c in range(chunks)
    ]
    loads[0].start()
    for copy in cot_loads:
        copy.start()
    for copy in loads[1:]:
        copy.start()

    def peer(k):
        other = lax.rem(flat + k + 1, ndev)
        return {"dp": lax.div(other, nmp), "mp": lax.rem(other, nmp)}

    barrier = pltpu.get_barrier_semaphore()
    loop(
        ndev - 1,
        lambda k: pl.semaphore_signal(
            barrier, inc=1, device_id=peer(k), device_id_type=MESH
        ),
    )

    def send_share(c):
        cols = pl.ds(c * width, width)

        def body(k):
            to = lax.rem(dp + k + 1, ndp)
            pltpu.make_async_remote_copy(
                src_ref=share.at[to, :, cols],
                dst_ref=grads.at[k, :, cols],
                send_sem=send_sem.at[0],
                recv_sem=recv_sem.at[0],
                device_id={"dp": to},
                device_id_type=MESH,
            ).start()

        return body

    loads[0].wait()
    for c in range(chunks):
        cot_loads[c].wait()
        part = lax.dot_general(
            hidden[...], cot[c], (((1,), (0,)), ((), ())), preferred_element_type=F32
        )
        for j in range(ndp):
            share[j, :, c * width : (c + 1) * width] = part[j * rows : (j + 1) * rows]
        if c == 0:
            pl.semaphore_wait(barrier, ndev - 1)
        loop(ndp - 1, send_share(c))

    for copy in loads[1:]:
        copy.wait()
    line = lax.broadcasted_iota(jnp.int32, (rows, ncols), 0)

    def row_scale(ref):
        scale = jnp.full((rows, ncols), ref[0], F32)
        for r in range(1, rows):
            scale = jnp.where(line == r, ref[r], scale)
        return scale

    level1 = (code1[...].astype(F32) - 7.5) / 7.5
    old1[...] = 0.9 * (level1 * jnp.minimum(row_scale(rows1_ref), cols1[...]))
    level2 = (code2[...].astype(F32) + 1.0) / 16.0
    old2[...] = 0.95 * (level2 * level2 * jnp.minimum(row_scale(rows2_ref), cols2[...]))
    steps = jnp.full((1, 128), step_ref[0], jnp.int32).astype(F32)
    fix1 = (1.0 - jnp.exp(steps * jnp.log(F32(0.9))))[:, :1]
    fix2 = (1.0 - jnp.exp(steps * jnp.log(F32(0.95))))[:, :1]

    def wait_all(ref, count, which):
        blocks = ref.at[pl.ds(0, count)]
        pltpu.make_async_copy(blocks, blocks, which).wait()

    wait_all(grads, ndp - 1, recv_sem.at[0])
    gradient = share[dp]
    if ndp <= 32:
        for k in range(ndp - 1):
            gradient += grads[k]
    else:
        gradient = lax.fori_loop(0, ndp - 1, lambda k, total: total + grads[k], gradient)

    lanes = jnp.sum(gradient * gradient, axis=0, keepdims=True)
    total = lanes[:, :128]
    for b in range(1, ncols // 128):
        total += lanes[:, b * 128 : (b + 1) * 128]
    square[0] = total

    def send_square(k):
        pltpu.make_async_remote_copy(
            src_ref=square.at[0],
            dst_ref=squares.at[k],
            send_sem=send_sem.at[1],
            recv_sem=recv_sem.at[1],
            device_id=peer(k),
            device_id_type=MESH,
        ).start()

    loop(ndev - 1, send_square)
    wait_all(squares, ndev - 1, recv_sem.at[1])
    total = total + jnp.sum(squares[...], axis=0)
    norm = jnp.sqrt(jnp.sum(total, axis=1, keepdims=True))
    entries = rows * ncols * ndev
    clipf = jnp.minimum(1.0, 0.01 * jnp.sqrt(F32(entries)) / (norm + 1e-6))
    clipped = clipf * gradient

    new1 = old1[...] + 0.1 * clipped
    new2 = old2[...] + 0.05 * (clipped * clipped)
    abs1 = jnp.abs(new1)
    maxcol[0, 0:1] = jnp.max(abs1, axis=0, keepdims=True)
    maxcol[0, 1:2] = jnp.max(new2, axis=0, keepdims=True)

    def send_cols(k):
        pltpu.make_async_remote_copy(
            src_ref=maxcol.at[0],
            dst_ref=maxcols.at[k],
            send_sem=send_sem.at[2],
            recv_sem=recv_sem.at[2],
            device_id={"dp": lax.rem(dp + k + 1, ndp)},
            device_id_type=MESH,
        ).start()

    loop(ndp - 1, send_cols)

    maxrow[0, 0] = jnp.broadcast_to(jnp.max(abs1, axis=1, keepdims=True), (rows, 128))
    maxrow[0, 1] = jnp.broadcast_to(jnp.max(new2, axis=1, keepdims=True), (rows, 128))

    def send_rows(k):
        pltpu.make_async_remote_copy(
            src_ref=maxrow.at[0],
            dst_ref=maxrows.at[k],
            send_sem=send_sem.at[3],
            recv_sem=recv_sem.at[3],
            device_id={"mp": lax.rem(mp + k + 1, nmp)},
            device_id_type=MESH,
        ).start()

    loop(nmp - 1, send_rows)

    ratio = new1 / fix1 / (jnp.sqrt(new2 / fix2) + 1e-8)
    weights = master[...]
    weights = weights - 0.001 * (ratio + 0.1 * weights)
    params[dp] = weights.astype(jnp.bfloat16)

    def send_params(k):
        pltpu.make_async_remote_copy(
            src_ref=params.at[dp],
            dst_ref=params.at[dp],
            send_sem=send_sem.at[4],
            recv_sem=recv_sem.at[4],
            device_id={"dp": lax.rem(dp + k + 1, ndp)},
            device_id_type=MESH,
        ).start()

    loop(ndp - 1, send_params)
    master_out[...] = weights
    ratio_out[...] = ratio

    wait_all(maxrows, nmp - 1, recv_sem.at[3])
    toprow = maxrow[0]
    for k in range(nmp - 1):
        toprow = jnp.maximum(toprow, maxrows[k])
    rows_out[...] = toprow
    wait_all(maxcols, ndp - 1, recv_sem.at[2])
    topcol = maxcol[0]
    if ndp <= 32:
        for k in range(ndp - 1):
            topcol = jnp.maximum(topcol, maxcols[k])
    else:
        topcol = lax.fori_loop(
            0, ndp - 1, lambda k, top: jnp.maximum(top, maxcols[k]), topcol
        )
    newcols1_out[...] = topcol[0:1]
    newcols2_out[...] = topcol[1:2]
    scaled1_out[...] = new1 / (jnp.minimum(toprow[0][:, :1], topcol[0:1]) + 1e-8)
    scaled2_out[...] = new2 / (jnp.minimum(toprow[1][:, :1], topcol[1:2]) + 1e-8)

    wait_all(params, ndp - 1, recv_sem.at[4])
    params_out[...] = params[...]

    wait_all(grads, ndp - 1, send_sem.at[0])
    wait_all(squares, ndev - 1, send_sem.at[1])
    wait_all(maxcols, ndp - 1, send_sem.at[2])
    wait_all(maxrows, nmp - 1, send_sem.at[3])
    wait_all(params, ndp - 1, send_sem.at[4])


def shards(
    ndp,
    nmp,
    hidden_input,
    output_cotangent,
    master_weights,
    first_codes,
    second_codes,
    first_rows,
    first_cols,
    second_rows,
    second_cols,
    step_count,
):
    rows, ncols = master_weights.shape
    tokens, width = hidden_input.shape
    chunks = 4
    anyspace = pl.BlockSpec(memory_space=pl.ANY)
    smem = pl.BlockSpec(memory_space=pltpu.SMEM)
    vmem = pl.BlockSpec(memory_space=pltpu.VMEM)
    whole = jax.ShapeDtypeStruct((rows, ncols), F32)
    line = jax.ShapeDtypeStruct((1, ncols), F32)
    outs = pl.pallas_call(
        functools.partial(kernel, ndp, nmp, chunks),
        out_shape=(
            whole,
            whole,
            jax.ShapeDtypeStruct((ndp, rows, ncols), jnp.bfloat16),
            whole,
            whole,
            jax.ShapeDtypeStruct((2, rows, 128), F32),
            line,
            line,
        ),
        in_specs=[anyspace] * 7 + [smem] * 3,
        out_specs=[vmem] * 8,
        scratch_shapes=[
            pltpu.VMEM((width, tokens), jnp.bfloat16),
            pltpu.VMEM((chunks, tokens, ncols // chunks), jnp.bfloat16),
            pltpu.VMEM((rows, ncols), F32),
            pltpu.VMEM((rows, ncols), jnp.int32),
            pltpu.VMEM((rows, ncols), jnp.int32),
            pltpu.VMEM((1, ncols), F32),
            pltpu.VMEM((1, ncols), F32),
            pltpu.VMEM((ndp, rows, ncols), F32),
            pltpu.VMEM((ndp - 1, rows, ncols), F32),
            pltpu.VMEM((1, 1, 128), F32),
            pltpu.VMEM((ndp * nmp - 1, 1, 128), F32),
            pltpu.VMEM((ndp, rows, ncols), jnp.bfloat16),
            pltpu.VMEM((1, 2, ncols), F32),
            pltpu.VMEM((ndp - 1, 2, ncols), F32),
            pltpu.VMEM((1, 2, rows, 128), F32),
            pltpu.VMEM((nmp - 1, 2, rows, 128), F32),
            pltpu.VMEM((rows, ncols), F32),
            pltpu.VMEM((rows, ncols), F32),
            pltpu.SemaphoreType.DMA((6,)),
            pltpu.SemaphoreType.DMA((chunks,)),
            pltpu.SemaphoreType.DMA((5,)),
            pltpu.SemaphoreType.DMA((5,)),
        ],
        compiler_params=pltpu.CompilerParams(
            collective_id=0, has_side_effects=True, vmem_limit_bytes=60 * 1024 * 1024
        ),
    )(
        hidden_input.T,
        output_cotangent,
        master_weights,
        first_codes,
        second_codes,
        first_cols.reshape(1, ncols),
        second_cols.reshape(1, ncols),
        first_rows,
        second_rows,
        step_count.reshape(1),
    )
    master, ratio, params, scaled1, scaled2, toprows, cols1, cols2 = outs
    return (
        master,
        ratio,
        params.reshape(ndp * rows, ncols),
        scaled1,
        scaled2,
        toprows[0, :, 0],
        cols1.reshape(ncols),
        toprows[1, :, 0],
        cols2.reshape(ncols),
    )


def solution(mesh):
    return jax.shard_map(
        functools.partial(shards, mesh.shape["dp"], mesh.shape["mp"]),
        mesh=mesh,
        in_specs=(
            P("dp", None),
            P("dp", "mp"),
            P("dp", "mp"),
            P("dp", "mp"),
            P("dp", "mp"),
            P("dp"),
            P("mp"),
            P("dp"),
            P("mp"),
            P(),
        ),
        out_specs=(
            P("dp", "mp"),
            P("dp", "mp"),
            P(None, "mp"),
            P("dp", "mp"),
            P("dp", "mp"),
            P("dp"),
            P("mp"),
            P("dp"),
            P("mp"),
        ),
        check_vma=False,
    )
```

time: 209 us -> 40.2 us (0.19)
  blocking collectives: 111 us -> 0 us
  waiting for transfers between devices: 70.8 us -> 0 us
  Pallas kernels: 0 us -> 27.3 us
  between operations: 15.7 us -> 1.3 us
  local copies, waits for them, and re-layouts: 2.81 us -> 11.1 us
  starting transfers between devices: 3.65 us -> 0 us
  matrix products: 3.52 us -> 0 us
    reduce_scatter x1 -> x0, waiting for transfers between devices: 64.8 us -> none  [shards(): lax.psum_scatter(whole_term, 'dp', scatter_dimension=1, tiled=True)]
    pmax x2 -> x0, blocking collectives: 42 us -> none  [the longest x1 35.4 us: shards(): lax.pmax((first_colpart, second_colpart), 'dp')]
    psum x1 -> x0, blocking collectives: 38.5 us -> none  [shards(): squares = lax.psum(jnp.sum(gradient * gradient), ('dp', 'mp'))]
    all_gather x1 -> x0, blocking collectives: 30.5 us -> none  [shards(): lax.all_gather(new_master.astype(jnp.bfloat16), 'dp', axis=0, tiled=True)]
    pallas_call x0 -> x1, Pallas kernels: none -> 27.3 us  [shards(): pl.pallas_call(functools.partial(kernel, ndp, nmp, chunks), out_shape=(wh...]
    unnamed x25 -> x6, local copies, waits for them, and re-layouts: 1.45 us -> 8.1 us
    all_to_all x1 -> x0, waiting for transfers between devices: 5.95 us -> none  [shards(): lax.all_to_all(column_share, 'dp', split_axis=0, concat_axis=1, tiled=True)]
    all_to_all x1 -> x0, starting transfers between devices: 3.61 us -> none  [shards(): lax.all_to_all(column_share, 'dp', split_axis=0, concat_axis=1, tiled=True)]
  transfers between devices with their start and end apart: 2 -> 0, of which waited for: 2 -> 0; matrix products, arithmetic and copies ran while one was open for 0% -> 0% of each run, Pallas kernels for 0% -> 0%
where the time goes in v1:
time: 40.2 us; the launch traced here: 39.7 us
  Pallas kernels  27.3 us (68%)
  local copies, waits for them, and re-layouts  11.1 us (28%)
  between operations  1.3 us (3%)
    pallas_call x1, Pallas kernels, shards(): pl.pallas_call(functools.partial(kernel, ndp, nmp, chunks), out_shape=(wh...  27.3 us
    unnamed x6, local copies, waits for them, and re-layouts  8.1 us
    reshape x1, local copies, waits for them, and re-layouts, shards(): params.reshape(ndp * rows, ncols)  1.63 us
    slice x1, local copies, waits for them, and re-layouts, shards(): toprows[1, :, 0]  1.35 us

profile of v1, /device:TPU:0, one launch (start us, length us, event | category | flops | bytes accessed | tf_op | source)
XLA Modules:
  0.0 39.7 jit_solution(6310594080090255876)
XLA Ops:
  1.3 27.3 %shard_map.169 = (f32[3,2048]{1,0:T(4,128)}, f32[3,2048]{1,0:T(4,128)}, bf16[8,3,2048]{2,1,0:T(4,128)(2,1)}, f32[3,2048]{1,0:T(4,128)}, f32[3,2048]{1,0:T(4,128)...) custom-call(bf16[24,1024]{1,0:T(8,128)(2,1)} %bitcast.7, bf16[1024,2048]{1,0:T(8,128)(2,1)} %cot_hbm.1, ...), custom_call_target="tpu_custom_call" | custom-call | tf_op jit(solution)/shard_map/pallas_call | solution.py:295
  28.6 1.3 %slice_reduce_fusion = (f32[3]{0:T(128)}, f32[3]{0:T(128)}) fusion(f32[2,3,128]{2,1,0:T(4,128)} %get-tuple-element.22), kind=kLoop, calls=%fused_computation | loop fusion | bytes 48 | tf_op jit(solution)/shard_map/slice | solution.py:357
  29.9 1.6 %reshape.39 = bf16[24,2048]{1,0:T(8,128)(2,1)} reshape(bf16[8,3,2048]{2,1,0:T(4,128)(2,1)} %get-tuple-element.19) | data formatting | bytes 196608 | tf_op jit(solution)/shard_map/reshape | solution.py:352
  31.6 1.4 %copy.26 = f32[3,2048]{1,0:T(4,128)} copy(f32[3,2048]{1,0:T(4,128)} %get-tuple-element.36) | data formatting | bytes 49152
  32.9 1.4 %copy.27 = f32[3,2048]{1,0:T(4,128)} copy(f32[3,2048]{1,0:T(4,128)} %get-tuple-element.37) | data formatting | bytes 49152
  34.3 1.4 %copy.28 = f32[3,2048]{1,0:T(4,128)} copy(f32[3,2048]{1,0:T(4,128)} %get-tuple-element.39) | data formatting | bytes 49152
  35.7 1.4 %copy.29 = f32[3,2048]{1,0:T(4,128)} copy(f32[3,2048]{1,0:T(4,128)} %get-tuple-element.40) | data formatting | bytes 49152
  37.1 1.3 %copy.30 = f32[2048]{0:T(1024)} copy(f32[2048]{0:T(1024)} %bitcast.11) | data formatting | bytes 16384
  38.4 1.3 %copy.31 = f32[2048]{0:T(1024)} copy(f32[2048]{0:T(1024)} %bitcast.10) | data formatting | bytes 16384

commit v2 on v1

v2 whole, which is shorter than its diff:
```python
import functools

import jax
import jax.numpy as jnp
from jax import lax
from jax.experimental import pallas as pl
from jax.experimental.pallas import tpu as pltpu
from jax.sharding import PartitionSpec as P

MESH = pl.DeviceIdType.MESH
F32 = jnp.float32


SUB = 8
LANES = 128


def kernel(
    ndp,
    nmp,
    loads_per_part,
    hidden_hbm,
    cot_hbm,
    master_hbm,
    code1_hbm,
    code2_hbm,
    cols1_hbm,
    cols2_hbm,
    rows1_hbm,
    rows2_hbm,
    step_hbm,
    master_out,
    ratio_out,
    params_out,
    scaled1_out,
    scaled2_out,
    rows_out,
    cols_out,
    hidden,
    cot,
    master,
    code1,
    code2,
    cols1,
    cols2,
    rows1,
    rows2,
    step_count,
    share,
    grads,
    square,
    squares,
    params,
    maxcol,
    maxcols,
    maxrow,
    maxrows,
    old1,
    old2,
    weights,
    in_sem,
    cot_sem,
    send_sem,
    recv_sem,
):
    dp = lax.axis_index("dp")
    mp = lax.axis_index("mp")
    ndev = ndp * nmp
    flat = dp * nmp + mp
    rows, ncols = master.shape
    parts = ncols // (SUB * LANES)
    deep = rows * SUB
    pieces = parts * loads_per_part
    width = ncols // pieces

    def loop(count, body):
        def step(i, carry):
            body(i)
            return carry

        lax.fori_loop(0, count, step, 0, unroll=count <= 32)

    loads = [
        pltpu.make_async_copy(src, dst, in_sem.at[i])
        for i, (src, dst) in enumerate(
            (
                (hidden_hbm, hidden),
                (code1_hbm, code1),
                (code2_hbm, code2),
                (cols1_hbm, cols1),
                (cols2_hbm, cols2),
                (master_hbm, master),
                (rows1_hbm, rows1),
                (rows2_hbm, rows2),
                (step_hbm, step_count),
            )
        )
    ]
    cot_loads = [
        pltpu.make_async_copy(
            cot_hbm.at[:, pl.ds(c * width, width)], cot.at[c], cot_sem.at[c]
        )
        for c in range(pieces)
    ]
    loads[0].start()
    for copy in cot_loads:
        copy.start()
    for copy in loads[1:]:
        copy.start()

    def peer(k):
        other = lax.rem(flat + k + 1, ndev)
        return {"dp": lax.div(other, nmp), "mp": lax.rem(other, nmp)}

    barrier = pltpu.get_barrier_semaphore()
    loop(
        ndev - 1,
        lambda k: pl.semaphore_signal(
            barrier, inc=1, device_id=peer(k), device_id_type=MESH
        ),
    )

    def send_share(p):
        def body(k):
            to = lax.rem(dp + k + 1, ndp)
            pltpu.make_async_remote_copy(
                src_ref=share.at[p, pl.ds(pl.multiple_of(to * deep, SUB), deep)],
                dst_ref=grads.at[k, pl.ds(p * deep, deep)],
                send_sem=send_sem.at[0],
                recv_sem=recv_sem.at[0],
                device_id={"dp": to},
                device_id_type=MESH,
            ).start()

        return body

    loads[0].wait()
    per_piece = width // LANES
    for c in range(pieces):
        cot_loads[c].wait()
        term = jnp.dot(hidden[...], cot[c], preferred_element_type=F32)
        p = c // loads_per_part
        for i in range(per_piece):
            sub = (c % loads_per_part) * per_piece + i
            share[p, pl.ds(sub, ndp * rows, stride=SUB), :] = term[
                :, i * LANES : (i + 1) * LANES
            ]
        if c == loads_per_part - 1:
            pl.semaphore_wait(barrier, ndev - 1)
        if c % loads_per_part == loads_per_part - 1:
            loop(ndp - 1, send_share(p))

    for copy in loads[1:]:
        copy.wait()

    def dense(value, ref):
        for b in range(ncols // LANES):
            at = (b // SUB) * deep + b % SUB
            ref[pl.ds(at, rows, stride=SUB), :] = value[:, b * LANES : (b + 1) * LANES]

    dense(code1[...].astype(F32), old1)
    dense(code2[...].astype(F32), old2)
    dense(master[...], weights)

    def scale(row_of, cols):
        tiles = []
        for p in range(parts):
            for r in range(rows):
                tiles.append(jnp.minimum(row_of(r), cols[p * SUB : (p + 1) * SUB]))
        return jnp.concatenate(tiles, axis=0)

    def tile(x, p, r):
        at = p * deep + r * SUB
        return x[at : at + SUB]

    level1 = (old1[...] - 7.5) / 7.5
    moment1 = 0.9 * (level1 * scale(lambda r: rows1[:, r : r + 1], cols1[...]))
    level2 = (old2[...] + 1.0) / 16.0
    moment2 = 0.95 * (level2 * level2 * scale(lambda r: rows2[:, r : r + 1], cols2[...]))
    steps = step_count[...].astype(F32)
    fix1 = 1.0 - jnp.exp(steps * jnp.log(F32(0.9)))
    fix2 = 1.0 - jnp.exp(steps * jnp.log(F32(0.95)))

    def wait_all(ref, count, which):
        blocks = ref.at[pl.ds(0, count)]
        pltpu.make_async_copy(blocks, blocks, which).wait()

    def fold(fn, first, ref, count):
        if count <= 32:
            for k in range(count):
                first = fn(first, ref[k])
            return first
        return lax.fori_loop(0, count, lambda k, x: fn(x, ref[k]), first)

    mine = pl.ds(pl.multiple_of(dp * deep, SUB), deep)
    gradient = jnp.concatenate([share[p, mine, :] for p in range(parts)], axis=0)
    wait_all(grads, ndp - 1, recv_sem.at[0])
    gradient = fold(jnp.add, gradient, grads, ndp - 1)

    lanes = jnp.sum(gradient * gradient, axis=0, keepdims=True)
    square[0] = lanes

    def send_square(k):
        pltpu.make_async_remote_copy(
            src_ref=square.at[0],
            dst_ref=squares.at[k],
            send_sem=send_sem.at[1],
            recv_sem=recv_sem.at[1],
            device_id=peer(k),
            device_id_type=MESH,
        ).start()

    loop(ndev - 1, send_square)
    wait_all(squares, ndev - 1, recv_sem.at[1])
    lanes = lanes + jnp.sum(squares[...], axis=0)
    norm = jnp.sqrt(jnp.sum(lanes, axis=1, keepdims=True))
    entries = rows * ncols * ndev
    clipf = jnp.minimum(1.0, 0.01 * jnp.sqrt(F32(entries)) / (norm + 1e-6))
    clipped = clipf * gradient

    new1 = moment1 + 0.1 * clipped
    new2 = moment2 + 0.05 * (clipped * clipped)
    abs1 = jnp.abs(new1)

    def over_rows(x):
        tops = []
        for p in range(parts):
            top = tile(x, p, 0)
            for r in range(1, rows):
                top = jnp.maximum(top, tile(x, p, r))
            tops.append(top)
        return jnp.concatenate(tops, axis=0)

    maxcol[0, 0] = over_rows(abs1)
    maxcol[0, 1] = over_rows(new2)

    def send_cols(k):
        pltpu.make_async_remote_copy(
            src_ref=maxcol.at[0],
            dst_ref=maxcols.at[k],
            send_sem=send_sem.at[2],
            recv_sem=recv_sem.at[2],
            device_id={"dp": lax.rem(dp + k + 1, ndp)},
            device_id_type=MESH,
        ).start()

    loop(ndp - 1, send_cols)

    ratio = new1 / fix1 / (jnp.sqrt(new2 / fix2) + 1e-8)
    old_weights = weights[...]
    new_weights = old_weights - 0.001 * (ratio + 0.1 * old_weights)
    params[dp] = new_weights.astype(jnp.bfloat16)

    def send_params(k):
        pltpu.make_async_remote_copy(
            src_ref=params.at[dp],
            dst_ref=params.at[dp],
            send_sem=send_sem.at[4],
            recv_sem=recv_sem.at[4],
            device_id={"dp": lax.rem(dp + k + 1, ndp)},
            device_id_type=MESH,
        ).start()

    loop(ndp - 1, send_params)

    def over_cols(x):
        tops = []
        for r in range(rows):
            top = tile(x, 0, r)
            for p in range(1, parts):
                top = jnp.maximum(top, tile(x, p, r))
            tops.append(jnp.max(top, axis=0, keepdims=True))
        return tops

    tops = jnp.concatenate(over_cols(abs1) + over_cols(new2), axis=0)
    maxrow[0] = jnp.broadcast_to(jnp.max(tops, axis=1, keepdims=True), tops.shape)

    def send_rows(k):
        pltpu.make_async_remote_copy(
            src_ref=maxrow.at[0],
            dst_ref=maxrows.at[k],
            send_sem=send_sem.at[3],
            recv_sem=recv_sem.at[3],
            device_id={"mp": lax.rem(mp + k + 1, nmp)},
            device_id_type=MESH,
        ).start()

    loop(nmp - 1, send_rows)
    master_out[...] = new_weights
    ratio_out[...] = ratio

    wait_all(maxrows, nmp - 1, recv_sem.at[3])
    toprow = fold(jnp.maximum, maxrow[0], maxrows, nmp - 1)
    rows_out[...] = toprow
    wait_all(maxcols, ndp - 1, recv_sem.at[2])
    topcol = fold(jnp.maximum, maxcol[0], maxcols, ndp - 1)
    cols_out[...] = topcol
    scaled1_out[...] = new1 / (scale(lambda r: toprow[r : r + 1], topcol[0]) + 1e-8)
    scaled2_out[...] = new2 / (
        scale(lambda r: toprow[rows + r : rows + r + 1], topcol[1]) + 1e-8
    )

    wait_all(params, ndp - 1, recv_sem.at[4])
    params_out[...] = params[...]

    wait_all(grads, ndp - 1, send_sem.at[0])
    wait_all(squares, ndev - 1, send_sem.at[1])
    wait_all(maxcols, ndp - 1, send_sem.at[2])
    wait_all(maxrows, nmp - 1, send_sem.at[3])
    wait_all(params, ndp - 1, send_sem.at[4])


def unpack(
    master,
    ratio,
    params,
    scaled1,
    scaled2,
    toprows,
    topcols,
    master_out,
    ratio_out,
    params_out,
    scaled1_out,
    scaled2_out,
    rows1_out,
    cols1_out,
    rows2_out,
    cols2_out,
    wide,
):
    rows, ncols = master_out.shape
    ndp = params.shape[0]
    parts = ncols // (SUB * LANES)
    deep = rows * SUB

    cols1_out[...] = topcols[0]
    cols2_out[...] = topcols[1]
    for r in range(rows):
        rows1_out[r] = jnp.max(toprows[r : r + 1, :])
        rows2_out[r] = jnp.max(toprows[rows + r : rows + r + 1, :])
    for j in range(ndp):
        block = params[j].astype(F32)
        for p in range(parts):
            wide[p, j * deep : (j + 1) * deep] = block[p * deep : (p + 1) * deep]
    for b in range(ncols // LANES):
        p, sub = b // SUB, b % SUB
        cols = slice(b * LANES, (b + 1) * LANES)
        part = pl.ds(p * deep + sub, rows, stride=SUB)
        master_out[:, cols] = master[part, :]
        ratio_out[:, cols] = ratio[part, :]
        scaled1_out[:, cols] = scaled1[part, :]
        scaled2_out[:, cols] = scaled2[part, :]
        params_out[:, cols] = wide[p, pl.ds(sub, ndp * rows, stride=SUB), :].astype(
            jnp.bfloat16
        )


def shards(
    ndp,
    nmp,
    hidden_input,
    output_cotangent,
    master_weights,
    first_codes,
    second_codes,
    first_rows,
    first_cols,
    second_rows,
    second_cols,
    step_count,
):
    rows, ncols = master_weights.shape
    tokens, width = hidden_input.shape
    parts = ncols // (SUB * LANES)
    loads = 2
    height = parts * rows * SUB
    hbm = pl.BlockSpec(memory_space=pltpu.HBM)
    smem = pl.BlockSpec(memory_space=pltpu.SMEM)
    vmem = pl.BlockSpec(memory_space=pltpu.VMEM)
    whole = jax.ShapeDtypeStruct((rows, ncols), F32)
    block = (height, LANES)
    line = (parts * SUB, LANES)
    dense = pltpu.VMEM(block, F32)
    results = pl.pallas_call(
        functools.partial(kernel, ndp, nmp, loads),
        out_shape=(
            dense,
            dense,
            pltpu.VMEM((ndp, *block), jnp.bfloat16),
            dense,
            dense,
            pltpu.VMEM((2 * rows, LANES), F32),
            pltpu.VMEM((2, *line), F32),
        ),
        in_specs=[hbm] * 10,
        out_specs=[vmem] * 7,
        scratch_shapes=[
            pltpu.VMEM((width, tokens), jnp.bfloat16),
            pltpu.VMEM((parts * loads, tokens, ncols // (parts * loads)), jnp.bfloat16),
            pltpu.VMEM((rows, ncols), F32),
            pltpu.VMEM((rows, ncols), jnp.int32),
            pltpu.VMEM((rows, ncols), jnp.int32),
            pltpu.VMEM(line, F32),
            pltpu.VMEM(line, F32),
            pltpu.VMEM((1, rows), F32),
            pltpu.VMEM((1, rows), F32),
            pltpu.VMEM((1, 1), jnp.int32),
            pltpu.VMEM((parts, ndp * rows * SUB, LANES), F32),
            pltpu.VMEM((ndp - 1, *block), F32),
            pltpu.VMEM((1, 1, LANES), F32),
            pltpu.VMEM((ndp * nmp - 1, 1, LANES), F32),
            pltpu.VMEM((ndp, *block), jnp.bfloat16),
            pltpu.VMEM((1, 2, *line), F32),
            pltpu.VMEM((ndp - 1, 2, *line), F32),
            pltpu.VMEM((1, 2 * rows, LANES), F32),
            pltpu.VMEM((nmp - 1, 2 * rows, LANES), F32),
            pltpu.VMEM(block, F32),
            pltpu.VMEM(block, F32),
            pltpu.VMEM(block, F32),
            pltpu.SemaphoreType.DMA((9,)),
            pltpu.SemaphoreType.DMA((parts * loads,)),
            pltpu.SemaphoreType.DMA((5,)),
            pltpu.SemaphoreType.DMA((5,)),
        ],
        compiler_params=pltpu.CompilerParams(
            collective_id=0, has_side_effects=True, vmem_limit_bytes=60 * 1024 * 1024
        ),
    )(
        hidden_input.T,
        output_cotangent,
        master_weights,
        first_codes,
        second_codes,
        first_cols.reshape(line),
        second_cols.reshape(line),
        first_rows.reshape(1, rows),
        second_rows.reshape(1, rows),
        step_count.reshape(1, 1),
    )
    scales = jax.ShapeDtypeStruct((rows,), F32)
    cols = jax.ShapeDtypeStruct(line, F32)
    outs = pl.pallas_call(
        unpack,
        out_shape=(
            whole,
            whole,
            jax.ShapeDtypeStruct((ndp * rows, ncols), jnp.bfloat16),
            whole,
            whole,
            scales,
            cols,
            scales,
            cols,
        ),
        in_specs=[vmem] * 7,
        out_specs=[vmem] * 5 + [smem, vmem] * 2,
        scratch_shapes=[pltpu.VMEM((parts, ndp * rows * SUB, LANES), F32)],
        compiler_params=pltpu.CompilerParams(vmem_limit_bytes=40 * 1024 * 1024),
    )(*results)
    return (*outs[:6], outs[6].reshape(ncols), outs[7], outs[8].reshape(ncols))


def solution(mesh):
    return jax.shard_map(
        functools.partial(shards, mesh.shape["dp"], mesh.shape["mp"]),
        mesh=mesh,
        in_specs=(
            P("dp", None),
            P("dp", "mp"),
            P("dp", "mp"),
            P("dp", "mp"),
            P("dp", "mp"),
            P("dp"),
            P("mp"),
            P("dp"),
            P("mp"),
            P(),
        ),
        out_specs=(
            P("dp", "mp"),
            P("dp", "mp"),
            P(None, "mp"),
            P("dp", "mp"),
            P("dp", "mp"),
            P("dp"),
            P("mp"),
            P("dp"),
            P("mp"),
        ),
        check_vma=False,
    )
```

time: 40.2 us -> 26.1 us (0.65)
  local copies, waits for them, and re-layouts: 11.1 us -> 0 us
  Pallas kernels: 27.3 us -> 24.7 us
    unnamed x6 -> x0, local copies, waits for them, and re-layouts: 8.1 us -> none
    pallas_call x1 -> x2, Pallas kernels: 27.3 us -> 24.7 us  [the longest x1 23.9 us: shards(): pl.pallas_call(functools.partial(kernel, ndp, nmp, loads), out_shape=(den...]
    reshape x1 -> x0, local copies, waits for them, and re-layouts: 1.63 us -> none  [shards(): params.reshape(ndp * rows, ncols)]
    slice x1 -> x0, local copies, waits for them, and re-layouts: 1.35 us -> none  [shards(): toprows[1, :, 0]]
where the time goes in v2:
time: 26.1 us; the launch traced here: 26 us
  Pallas kernels  24.7 us (95%)
  between operations  1.3 us (5%)
    pallas_call x1, Pallas kernels, shards(): pl.pallas_call(functools.partial(kernel, ndp, nmp, loads), out_shape=(den...  23.9 us
    pallas_call x1, Pallas kernels, shards(): pl.pallas_call(unpack, out_shape=(whole, whole, jax.ShapeDtypeStruct((ndp...  0.76 us

profile of v2, /device:TPU:0, one launch (start us, length us, event | category | flops | bytes accessed | tf_op | source)
XLA Modules:
  0.0 26.0 jit_solution(17265167013010662991)
XLA Ops:
  1.3 23.9 %shard_map.169 = (f32[48,128]{1,0:T(8,128)S(1)}, f32[48,128]{1,0:T(8,128)S(1)}, bf16[8,48,128]{2,1,0:T(8,128)(2,1)S(1)}, f32[48,128]{1,0:T(8,128)S(1)}, f32[48,1...) custom-call(bf16[24,1024]{1,0:T(8,128)(2,1)} %bitcast.9, bf16[1024,2048]{1,0:T(8,128)(2,1)} %cot_hbm.1, ...), custom_call_target="tpu_custom_call" | custom-call | tf_op jit(solution)/shard_map/pallas_call | solution.py:385
  25.2 0.8 %shard_map.170 = (f32[3,2048]{1,0:T(4,128)}, f32[3,2048]{1,0:T(4,128)}, bf16[24,2048]{1,0:T(8,128)(2,1)}, f32[3,2048]{1,0:T(4,128)}, f32[3,2048]{1,0:T(4,128)}, ...) custom-call(f32[48,128]{1,0:T(8,128)S(1)} %get-tuple-element.25.master, ...), custom_call_target="tpu_custom_call" | custom-call | tf_op jit(solution)/shard_map/pallas_call | solution.py:443

commit v3 on v2

--- a/solution.py
+++ b/solution.py
@@ -234,17 +234,15 @@
     maxcol[0, 0] = over_rows(abs1)
     maxcol[0, 1] = over_rows(new2)
 
-    def send_cols(k):
-        pltpu.make_async_remote_copy(
-            src_ref=maxcol.at[0],
-            dst_ref=maxcols.at[k],
-            send_sem=send_sem.at[2],
-            recv_sem=recv_sem.at[2],
-            device_id={"dp": lax.rem(dp + k + 1, ndp)},
-            device_id_type=MESH,
-        ).start()
-
-    loop(ndp - 1, send_cols)
+    pair = pltpu.make_async_remote_copy(
+        src_ref=maxcol.at[0],
+        dst_ref=maxcol.at[1],
+        send_sem=send_sem.at[5],
+        recv_sem=recv_sem.at[5],
+        device_id={"dp": dp + 1 - 2 * lax.rem(dp, 2)},
+        device_id_type=MESH,
+    )
+    pair.start()
 
     ratio = new1 / fix1 / (jnp.sqrt(new2 / fix2) + 1e-8)
     old_weights = weights[...]
@@ -286,14 +284,28 @@
         ).start()
 
     loop(nmp - 1, send_rows)
+
+    def send_cols(k):
+        pltpu.make_async_remote_copy(
+            src_ref=maxcol.at[2],
+            dst_ref=maxcols.at[k],
+            send_sem=send_sem.at[2],
+            recv_sem=recv_sem.at[2],
+            device_id={"dp": lax.rem(dp + 2 * (k + 1), ndp)},
+            device_id_type=MESH,
+        ).start()
+
+    pair.wait_recv()
+    maxcol[2] = jnp.maximum(maxcol[0], maxcol[1])
+    loop(ndp // 2 - 1, send_cols)
     master_out[...] = new_weights
     ratio_out[...] = ratio
 
     wait_all(maxrows, nmp - 1, recv_sem.at[3])
     toprow = fold(jnp.maximum, maxrow[0], maxrows, nmp - 1)
     rows_out[...] = toprow
-    wait_all(maxcols, ndp - 1, recv_sem.at[2])
-    topcol = fold(jnp.maximum, maxcol[0], maxcols, ndp - 1)
+    wait_all(maxcols, ndp // 2 - 1, recv_sem.at[2])
+    topcol = fold(jnp.maximum, maxcol[2], maxcols, ndp // 2 - 1)
     cols_out[...] = topcol
     scaled1_out[...] = new1 / (scale(lambda r: toprow[r : r + 1], topcol[0]) + 1e-8)
     scaled2_out[...] = new2 / (
@@ -305,7 +317,8 @@
 
     wait_all(grads, ndp - 1, send_sem.at[0])
     wait_all(squares, ndev - 1, send_sem.at[1])
-    wait_all(maxcols, ndp - 1, send_sem.at[2])
+    pair.wait_send()
+    wait_all(maxcols, ndp // 2 - 1, send_sem.at[2])
     wait_all(maxrows, nmp - 1, send_sem.at[3])
     wait_all(params, ndp - 1, send_sem.at[4])
 
@@ -411,8 +424,8 @@
             pltpu.VMEM((1, 1, LANES), F32),
             pltpu.VMEM((ndp * nmp - 1, 1, LANES), F32),
             pltpu.VMEM((ndp, *block), jnp.bfloat16),
-            pltpu.VMEM((1, 2, *line), F32),
-            pltpu.VMEM((ndp - 1, 2, *line), F32),
+            pltpu.VMEM((3, 2, *line), F32),
+            pltpu.VMEM((ndp // 2 - 1, 2, *line), F32),
             pltpu.VMEM((1, 2 * rows, LANES), F32),
             pltpu.VMEM((nmp - 1, 2 * rows, LANES), F32),
             pltpu.VMEM(block, F32),
@@ -420,8 +433,8 @@
             pltpu.VMEM(block, F32),
             pltpu.SemaphoreType.DMA((9,)),
             pltpu.SemaphoreType.DMA((parts * loads,)),
-            pltpu.SemaphoreType.DMA((5,)),
-            pltpu.SemaphoreType.DMA((5,)),
+            pltpu.SemaphoreType.DMA((6,)),
+            pltpu.SemaphoreType.DMA((6,)),
         ],
         compiler_params=pltpu.CompilerParams(
             collective_id=0, has_side_effects=True, vmem_limit_bytes=60 * 1024 * 1024

time: 26.1 us -> 25.6 us (0.981)
  Pallas kernels: 24.7 us -> 24.1 us
    pallas_call x1, Pallas kernels: 23.9 us -> 23.4 us  [shards(): pl.pallas_call(functools.partial(kernel, ndp, nmp, loads), out_shape=(den...]
where the time goes in v3:
time: 25.6 us; the launch traced here: 25.4 us
  Pallas kernels  24.1 us (94%)
  between operations  1.3 us (5%)
    pallas_call x1, Pallas kernels, shards(): pl.pallas_call(functools.partial(kernel, ndp, nmp, loads), out_shape=(den...  23.4 us
    pallas_call x1, Pallas kernels, shards(): pl.pallas_call(unpack, out_shape=(whole, whole, jax.ShapeDtypeStruct((ndp...  0.76 us

profile of v3, /device:TPU:0, one launch (start us, length us, event | category | flops | bytes accessed | tf_op | source)
XLA Modules:
  0.0 25.4 jit_solution(9781139177684148785)
XLA Ops:
  1.3 23.4 %shard_map.169 = (f32[48,128]{1,0:T(8,128)S(1)}, f32[48,128]{1,0:T(8,128)S(1)}, bf16[8,48,128]{2,1,0:T(8,128)(2,1)S(1)}, f32[48,128]{1,0:T(8,128)S(1)}, f32[48,1...) custom-call(bf16[24,1024]{1,0:T(8,128)(2,1)} %bitcast.9, bf16[1024,2048]{1,0:T(8,128)(2,1)} %cot_hbm.1, ...), custom_call_target="tpu_custom_call" | custom-call | tf_op jit(solution)/shard_map/pallas_call | solution.py:398
  24.7 0.8 %shard_map.170 = (f32[3,2048]{1,0:T(4,128)}, f32[3,2048]{1,0:T(4,128)}, bf16[24,2048]{1,0:T(8,128)(2,1)}, f32[3,2048]{1,0:T(4,128)}, f32[3,2048]{1,0:T(4,128)}, ...) custom-call(f32[48,128]{1,0:T(8,128)S(1)} %get-tuple-element.25.master, ...), custom_call_target="tpu_custom_call" | custom-call | tf_op jit(solution)/shard_map/pallas_call | solution.py:456

commit v4 on v3

--- a/solution.py
+++ b/solution.py
@@ -102,12 +102,6 @@
         )
         for c in range(pieces)
     ]
-    loads[0].start()
-    for copy in cot_loads:
-        copy.start()
-    for copy in loads[1:]:
-        copy.start()
-
     def peer(k):
         other = lax.rem(flat + k + 1, ndev)
         return {"dp": lax.div(other, nmp), "mp": lax.rem(other, nmp)}
@@ -119,6 +113,12 @@
             barrier, inc=1, device_id=peer(k), device_id_type=MESH
         ),
     )
+
+    loads[0].start()
+    for copy in cot_loads:
+        copy.start()
+    for copy in loads[1:]:
+        copy.start()
 
     def send_share(p):
         def body(k):
@@ -203,10 +203,10 @@
     def send_square(k):
         pltpu.make_async_remote_copy(
             src_ref=square.at[0],
-            dst_ref=squares.at[k],
+            dst_ref=squares.at[ndev - 2 - k],
             send_sem=send_sem.at[1],
             recv_sem=recv_sem.at[1],
-            device_id=peer(k),
+            device_id=peer(ndev - 2 - k),
             device_id_type=MESH,
         ).start()
 
@@ -244,6 +244,30 @@
     )
     pair.start()
 
+    def over_cols(x):
+        tops = []
+        for r in range(rows):
+            top = tile(x, 0, r)
+            for p in range(1, parts):
+                top = jnp.maximum(top, tile(x, p, r))
+            tops.append(jnp.max(top, axis=0, keepdims=True))
+        return tops
+
+    tops = jnp.concatenate(over_cols(abs1) + over_cols(new2), axis=0)
+    maxrow[0] = jnp.broadcast_to(jnp.max(tops, axis=1, keepdims=True), tops.shape)
+
+    def send_rows(k):
+        pltpu.make_async_remote_copy(
+            src_ref=maxrow.at[0],
+            dst_ref=maxrows.at[k],
+            send_sem=send_sem.at[3],
+            recv_sem=recv_sem.at[3],
+            device_id={"mp": lax.rem(mp + k + 1, nmp)},
+            device_id_type=MESH,
+        ).start()
+
+    loop(nmp - 1, send_rows)
+
     ratio = new1 / fix1 / (jnp.sqrt(new2 / fix2) + 1e-8)
     old_weights = weights[...]
     new_weights = old_weights - 0.001 * (ratio + 0.1 * old_weights)
@@ -261,29 +285,6 @@
 
     loop(ndp - 1, send_params)
 
-    def over_cols(x):
-        tops = []
-        for r in range(rows):
-            top = tile(x, 0, r)
-            for p in range(1, parts):
-                top = jnp.maximum(top, tile(x, p, r))
-            tops.append(jnp.max(top, axis=0, keepdims=True))
-        return tops
-
-    tops = jnp.concatenate(over_cols(abs1) + over_cols(new2), axis=0)
-    maxrow[0] = jnp.broadcast_to(jnp.max(tops, axis=1, keepdims=True), tops.shape)
-
-    def send_rows(k):
-        pltpu.make_async_remote_copy(
-            src_ref=maxrow.at[0],
-            dst_ref=maxrows.at[k],
-            send_sem=send_sem.at[3],
-            recv_sem=recv_sem.at[3],
-            device_id={"mp": lax.rem(mp + k + 1, nmp)},
-            device_id_type=MESH,
-        ).start()
-
-    loop(nmp - 1, send_rows)
 
     def send_cols(k):
         pltpu.make_async_remote_copy(

time: 25.6 us -> 25.5 us (level)
  no operation moved by 1% of the time
where the time goes in v4:
time: 25.5 us; the launch traced here: 25.4 us
  Pallas kernels  24.1 us (95%)
  between operations  1.3 us (5%)
    pallas_call x1, Pallas kernels, shards(): pl.pallas_call(functools.partial(kernel, ndp, nmp, loads), out_shape=(den...  23.3 us
    pallas_call x1, Pallas kernels, shards(): pl.pallas_call(unpack, out_shape=(whole, whole, jax.ShapeDtypeStruct((ndp...  0.76 us

profile of v4, /device:TPU:0, one launch (start us, length us, event | category | flops | bytes accessed | tf_op | source)
XLA Modules:
  0.0 25.4 jit_solution(2566520712415103571)
XLA Ops:
  1.3 23.3 %shard_map.169 = (f32[48,128]{1,0:T(8,128)S(1)}, f32[48,128]{1,0:T(8,128)S(1)}, bf16[8,48,128]{2,1,0:T(8,128)(2,1)S(1)}, f32[48,128]{1,0:T(8,128)S(1)}, f32[48,1...) custom-call(bf16[24,1024]{1,0:T(8,128)(2,1)} %bitcast.9, bf16[1024,2048]{1,0:T(8,128)(2,1)} %cot_hbm.1, ...), custom_call_target="tpu_custom_call" | custom-call | tf_op jit(solution)/shard_map/pallas_call | solution.py:399
  24.6 0.8 %shard_map.170 = (f32[3,2048]{1,0:T(4,128)}, f32[3,2048]{1,0:T(4,128)}, bf16[24,2048]{1,0:T(8,128)(2,1)}, f32[3,2048]{1,0:T(4,128)}, f32[3,2048]{1,0:T(4,128)}, ...) custom-call(f32[48,128]{1,0:T(8,128)S(1)} %get-tuple-element.25.master, ...), custom_call_target="tpu_custom_call" | custom-call | tf_op jit(solution)/shard_map/pallas_call | solution.py:457
